TPU v7x, 256 devices: a whole 4x4x8 slice. The times are simulated.
256 devices in a mesh: gx: 16 (over z, x_lo), gy: 4 (over y), gz: 4 (over x_hi, core).
Axes of the slice: x: 4 (x_hi: 2, x_lo: 2; x = x_hi * 2 + x_lo), y: 4, z: 8, core: 2. Of those that a mesh axis runs over, the one named last changes fastest.
Arguments:
- state: float32 [5, 96, 96, 1536], P(None, 'gx', 'gy', 'gz'), as said below
- register: float32 [5, 96, 96, 1536], P(None, 'gx', 'gy', 'gz'), may hold values from -0.25 to 0.25
Outputs:
- new_state: float32 [5, 96, 96, 1536], P(None, 'gx', 'gy', 'gz')
- new_register: float32 [5, 96, 96, 1536], P(None, 'gx', 'gy', 'gz')
Inputs may be any that keep to these rules, and one draw needn't show every extreme that they name: Density is between 0.5 and 2.5, and the pressure computed from the state is positive.
All inputs are finite; a program needn't handle non-finite values.
Results may differ from a plain program's by a relative error of at most 0.0003.
Values sent between devices are 32-bit elements; how exact they have to be, the bound alone decides.
A program may use at most 128 MiB of HBM per device.

v0:
```python
import functools
import math

import jax
import jax.numpy as jnp
import numpy as np
from jax import lax
from jax.experimental import pallas as pl
from jax.experimental.pallas import tpu as pltpu
from jax.sharding import Mesh
from jax.sharding import PartitionSpec as P

AXES = ("gx_0", "gx_1", "gy", "gz_0", "gz_1")
MESH = pl.DeviceIdType.MESH

GAMMA = 1.4
GM1 = 0.4
ELEM_WIDTH = 0.05
COURANT = 0.5
COEFFS = (
    (-567301805773.0 / 1357537059087.0, 5161836677717.0 / 13612068292357.0),
    (-2404267990393.0 / 2016746695238.0, 1720146321549.0 / 2090206949498.0),
)
NV = 5
N = 6
NX, NY, NZ = 6, 24, 384
ROWS = 8
CH = NY // ROWS
LANES = 128
SCALE = 2.0 / ELEM_WIDTH
FACE = SCALE * 15.0 * 0.5


def gll_derivative():
    seven = math.sqrt(7.0)
    inner = math.sqrt(1.0 / 3.0 - 2.0 * seven / 21.0)
    outer = math.sqrt(1.0 / 3.0 + 2.0 * seven / 21.0)
    points = np.array([-1.0, -outer, -inner, inner, outer, 1.0])
    count = len(points)
    weights = np.array(
        [np.prod([points[i] - points[j] for j in range(count) if j != i]) for i in range(count)]
    )
    table = np.zeros((count, count))
    for i in range(count):
        for j in range(count):
            if i != j:
                table[i, j] = weights[i] / weights[j] / (points[i] - points[j])
        table[i, i] = -np.sum(table[i])
    return table


DIFF = gll_derivative()


def line_operator(length):
    elems = length // N
    op = np.kron(np.eye(elems), -SCALE * DIFF)
    for e in range(elems - 1):
        last, first = N * e + N - 1, N * e + N
        for row in (last, first):
            op[row, last] += FACE
            op[row, first] -= FACE
    return op


def operators():
    along_z = line_operator(NZ).T
    cut = 2 * LANES - (2 * LANES) % N
    low = along_z[: 2 * LANES, : 2 * LANES].copy()
    low[:, cut:] = 0.0
    high = along_z[LANES:, LANES:].copy()
    high[:, : cut - LANES] = 0.0
    along_y = np.kron(np.eye(NX), line_operator(NY))
    return (
        jnp.asarray(np.stack([low, high]), jnp.float32),
        jnp.asarray(along_y, jnp.float32),
    )


def primitives(u):
    inv = 1.0 / u[0]
    vel = [u[1] * inv, u[2] * inv, u[3] * inv]
    press = GM1 * (u[4] - 0.5 * (u[1] * vel[0] + u[2] * vel[1] + u[3] * vel[2]))
    sound = jnp.sqrt(GAMMA * press * inv)
    return vel, press, sound


def flux(u, vel, press, d):
    parts = [u[1 + d], u[1] * vel[d], u[2] * vel[d], u[3] * vel[d], (u[4] + press) * vel[d]]
    parts[1 + d] = parts[1 + d] + press
    return parts


def face_terms(left, right, d):
    vel_l, press_l, sound_l = primitives(left)
    vel_r, press_r, sound_r = primitives(right)
    flux_l = flux(left, vel_l, press_l, d)
    flux_r = flux(right, vel_r, press_r, d)
    lam = FACE * jnp.maximum(jnp.abs(vel_l[d]) + sound_l, jnp.abs(vel_r[d]) + sound_r)
    a = [FACE * (fl - fr) for fl, fr in zip(flux_l, flux_r)]
    b = [lam * (r - l) for l, r in zip(left, right)]
    return a, b


def kernel(
    sizes,
    state,
    register,
    mat_z,
    mat_y,
    out_state,
    out_register,
    u,
    k,
    res,
    fx,
    fy,
    fz,
    mz,
    my,
    mask_z,
    step,
    top,
    top_x,
    top_z,
    top_y,
    y_pack,
    z_pack,
    y_halo,
    z_halo,
    x_halo,
    y_corr,
    z_corr,
    load_sem,
    send_x,
    recv_x,
    send_yz,
    recv_yz,
    send_top,
    recv_top,
):
    nz, nxl, ny, nxh, nco = sizes
    z, xl, y, xh, co = (lax.axis_index(a) for a in AXES)

    def device(z_=z, xl_=xl, y_=y, xh_=xh, co_=co):
        return dict(zip(AXES, (z_, xl_, y_, xh_, co_)))

    def wrap(i, n):
        return lax.rem(i + n, n)

    other_xl, other_co = wrap(xl + 1, nxl), wrap(co + 1, nco)
    gx = (
        device(z_=wrap(z + xl - 1, nz), xl_=other_xl),
        device(z_=wrap(z + xl, nz), xl_=other_xl),
    )
    gy = (device(y_=wrap(y - 1, ny)), device(y_=wrap(y + 1, ny)))
    gz = (
        device(xh_=wrap(xh + co - 1, nxh), co_=other_co),
        device(xh_=wrap(xh + co, nxh), co_=other_co),
    )
    group_x = [
        device(xh_=wrap(xh + a, nxh), xl_=wrap(xl + b, nxl), co_=wrap(co + c, nco))
        for a in range(nxh)
        for b in range(nxl)
        for c in range(nco)
        if a or b or c
    ]
    group_z = [device(z_=wrap(z + i, nz)) for i in range(1, nz)]
    group_y = [device(y_=wrap(y + i, ny)) for i in range(1, ny)]
    diagonal = device(z_=wrap(z + 2 * xl - 1, nz), xl_=other_xl)

    loads = [
        pltpu.make_async_copy(state, u, load_sem.at[0]),
        pltpu.make_async_copy(register, k, load_sem.at[1]),
        pltpu.make_async_copy(mat_z, mz, load_sem.at[2]),
        pltpu.make_async_copy(mat_y, my, load_sem.at[3]),
    ]
    for load in loads:
        load.start()
    barrier = pltpu.get_barrier_semaphore()
    partners = group_x + group_z + group_y + [diagonal]
    for partner in partners:
        pl.semaphore_signal(barrier, inc=1, device_id=partner, device_id_type=MESH)

    lane = lax.broadcasted_iota(jnp.int32, (ROWS, NZ), 1)
    lane_f = lane.astype(jnp.float32)
    place = lane_f - N * jnp.floor((lane_f + 0.5) * (1.0 / N))
    mask_z[...] = jnp.where((place > N - 1.5) & (lane < NZ - 1), FACE, 0.0)
    row = lax.broadcasted_iota(jnp.int32, (ROWS, NZ), 0)
    lane_1 = lax.broadcasted_iota(jnp.int32, (NY, LANES), 1)

    def chunk(ref, x, c):
        return [ref[v, x, pl.ds(ROWS * c, ROWS), :] for v in range(NV)]

    loads[0].wait()
    top[0] = jnp.zeros((ROWS, LANES), jnp.float32)

    def speed_body(x, carry):
        for c in range(CH):
            w = chunk(u, x, c)
            vel, press, sound = primitives(w)
            mom = jnp.sqrt(w[1] * w[1] + w[2] * w[2] + w[3] * w[3])
            s = mom * (1.0 / w[0]) + sound
            carry = jnp.maximum(carry, s)
        return carry

    best = lax.fori_loop(0, NX, speed_body, jnp.zeros((ROWS, NZ), jnp.float32))
    top[0] = jnp.maximum(
        jnp.maximum(best[:, :LANES], best[:, LANES : 2 * LANES]), best[:, 2 * LANES :]
    )

    def pack(sec):
        def body(v, carry):
            low, high = carry
            for x in range(NX):
                y_pack[sec, 0, v, x : x + 1, :] = u[v, x, 0:1, :]
                y_pack[sec, 1, v, x : x + 1, :] = u[v, x, NY - 1 : NY, :]
                here = lane_1 == v * NX + x
                low = jnp.where(here, u[v, x, :, 0:LANES][:, 0:1], low)
                high = jnp.where(here, u[v, x, :, NZ - LANES : NZ][:, LANES - 1 : LANES], high)
            for x in range(NX, ROWS):
                y_pack[sec, 0, v, x : x + 1, :] = u[v, 0, 0:1, :]
                y_pack[sec, 1, v, x : x + 1, :] = u[v, 0, NY - 1 : NY, :]
            return low, high

        ones = jnp.ones((NY, LANES), jnp.float32)
        low, high = lax.fori_loop(0, NV, body, (ones, ones))
        z_pack[sec, 0] = low
        z_pack[sec, 1] = high

    def remote(src, dst, send, recv, to):
        return pltpu.make_async_remote_copy(
            src_ref=src,
            dst_ref=dst,
            send_sem=send,
            recv_sem=recv,
            device_id=to,
            device_id_type=MESH,
        )

    def x_copy(sec, side, c):
        src = state if sec == 0 else u
        return remote(
            src.at[:, 0 if side == 0 else NX - 1, pl.ds(ROWS * c, ROWS), :],
            x_halo.at[sec, 1 - side, c],
            send_x.at[sec, side, c],
            recv_x.at[sec, 1 - side, c],
            gx[side],
        )

    def y_copy(sec, side):
        return remote(
            y_pack.at[sec, side],
            y_halo.at[sec, 1 - side],
            send_yz.at[sec, 0, side],
            recv_yz.at[sec, 0, 1 - side],
            gy[side],
        )

    def z_copy(sec, side):
        return remote(
            z_pack.at[sec, side],
            z_halo.at[sec, 1 - side],
            send_yz.at[sec, 1, side],
            recv_yz.at[sec, 1, 1 - side],
            gz[side],
        )

    def top_copies(stage, group, slots, first):
        return [
            remote(top.at[stage], slots.at[i], send_top.at[first + i], recv_top.at[first + i], to)
            for i, to in enumerate(group)
        ]

    tops_x = top_copies(0, group_x, top_x, 0)
    tops_z = top_copies(1, group_z, top_z, len(group_x))
    tops_y = top_copies(2, group_y, top_y, len(group_x) + len(group_z))

    def start(copies):
        for copy in copies:
            copy.start()

    def gather_top(stage, copies, slots):
        value = top[stage]
        for i, copy in enumerate(copies):
            copy.wait_recv()
            value = jnp.maximum(value, slots[i])
        return value

    def y_z_copies(sec):
        return [z_copy(sec, 0), z_copy(sec, 1), y_copy(sec, 0), y_copy(sec, 1)]

    def fluxes_and_jumps():
        def body(x, carry):
            for c in range(CH):
                w = chunk(u, x, c)
                vel, press, sound = primitives(w)
                rows = pl.ds(ROWS * c, ROWS)
                for d, to in enumerate((fx, fy, fz)):
                    for v, part in enumerate(flux(w, vel, press, d)):
                        to[v, x, rows, :] = part
                s_y = jnp.abs(vel[1]) + sound
                s_z = jnp.abs(vel[2]) + sound
                lam_y = jnp.where(
                    row == N - 1 - 2 * c,
                    FACE * jnp.maximum(s_y, pltpu.roll(s_y, ROWS - 1, 0)),
                    0.0,
                )
                lam_z = mask_z[...] * jnp.maximum(s_z, pltpu.roll(s_z, NZ - 1, 1))
                for v in range(NV):
                    t_y = lam_y * (pltpu.roll(w[v], ROWS - 1, 0) - w[v])
                    t_z = lam_z * (pltpu.roll(w[v], NZ - 1, 1) - w[v])
                    res[v, x, rows, :] = (t_y - pltpu.roll(t_y, 1, 0)) + (
                        t_z - pltpu.roll(t_z, 1, 1)
                    )
            return carry

        lax.fori_loop(0, NX, body, 0)

    def dot(a, b):
        return jnp.dot(
            a, b, precision=lax.Precision.HIGHEST, preferred_element_type=jnp.float32
        )

    def lines_y_z():
        def body(v, carry):
            along_z = fz[v].reshape(NX * NY, NZ)
            low = dot(along_z[:, : 2 * LANES], mz[0])
            high = dot(along_z[:, LANES:], mz[1])
            both = jnp.concatenate(
                [low[:, :LANES], low[:, LANES:] + high[:, :LANES], high[:, LANES:]], axis=1
            )
            along_y = dot(my[...], fy[v].reshape(NX * NY, NZ))
            res[v] = res[v] + (both + along_y).reshape(NX, NY, NZ)
            return carry

        lax.fori_loop(0, NV, body, 0)

    def lines_x():
        half = N // 2
        even = [[-SCALE * 0.5 * (DIFF[i, j] + DIFF[i, N - 1 - j]) for j in range(half)] for i in range(half)]
        odd = [[-SCALE * 0.5 * (DIFF[i, j] - DIFF[i, N - 1 - j]) for j in range(half)] for i in range(half)]

        def body(v, carry):
            for c in range(CH):
                rows = pl.ds(ROWS * c, ROWS)
                f = [fx[v, x, rows, :] for x in range(NX)]
                plus = [f[j] + f[N - 1 - j] for j in range(half)]
                minus = [f[j] - f[N - 1 - j] for j in range(half)]
                for i in range(half):
                    a = sum(even[i][j] * plus[j] for j in range(half))
                    b = sum(odd[i][j] * minus[j] for j in range(half))
                    res[v, i, rows, :] += b + a
                    res[v, N - 1 - i, rows, :] += b - a
            return carry

        lax.fori_loop(0, NV, body, 0)

    def y_z_faces(sec):
        for side in (0, 1):
            y_copy(sec, 1 - side).wait_recv()
            own = [y_pack[sec, side, v] for v in range(NV)]
            far = [y_halo[sec, side, v] for v in range(NV)]
            a, b = face_terms(far, own, 1) if side == 0 else face_terms(own, far, 1)
            for v in range(NV):
                y_corr[side, v] = a[v] - b[v] if side == 0 else a[v] + b[v]
            z_copy(sec, 1 - side).wait_recv()

            def part(ref, v):
                tile = ref[sec, side]
                return tile if v == 0 else pltpu.roll(tile, LANES - NX * v, 1)

            own = [part(z_pack, v) for v in range(NV)]
            far = [part(z_halo, v) for v in range(NV)]
            a, b = face_terms(far, own, 2) if side == 0 else face_terms(own, far, 2)
            for v in range(NV):
                z_corr[side, v] = a[v] - b[v] if side == 0 else a[v] + b[v]

        def body(v, carry):
            for x in range(NX):
                res[v, x, 0:1, :] += y_corr[0, v, x : x + 1, :]
                res[v, x, NY - 1 : NY, :] += y_corr[1, v, x : x + 1, :]
                low = z_corr[0, v][:, x : x + 1]
                high = z_corr[1, v][:, x : x + 1]
                res[v, x, :, 0:LANES] += jnp.where(lane_1 == 0, low, 0.0)
                res[v, x, :, NZ - LANES : NZ] += jnp.where(lane_1 == LANES - 1, high, 0.0)
            return carry

        lax.fori_loop(0, NV, body, 0)

    def interior(sec):
        fluxes_and_jumps()
        if sec == 0:
            value = gather_top(0, tops_x, top_x)
            top[1] = value
            start(tops_z)
            loads[2].wait()
            loads[3].wait()
        lines_y_z()
        lines_x()
        y_z_faces(sec)

    def update(sec, x, c, extra):
        a, b = COEFFS[sec]
        rows = pl.ds(ROWS * c, ROWS)
        dt = step[...]
        for v in range(NV):
            r = res[v, x, rows, :]
            if extra is not None:
                r = r + extra[v]
            new_k = a * k[v, x, rows, :] + dt * r
            new_u = u[v, x, rows, :] + b * new_k
            if sec == 0:
                k[v, x, rows, :] = new_k
                u[v, x, rows, :] = new_u
            else:
                out_register[v, x, rows, :] = new_k
                out_state[v, x, rows, :] = new_u

    def update_boundary(sec, side, c):
        x_copy(sec, 1 - side, c).wait_recv()
        x = 0 if side == 0 else NX - 1
        own = chunk(u, x, c)
        far = [x_halo[sec, side, c, v] for v in range(NV)]
        a, b = face_terms(far, own, 0) if side == 0 else face_terms(own, far, 0)
        extra = [p - q if side == 0 else p + q for p, q in zip(a, b)]
        update(sec, x, c, extra)

    def update_interior(sec):
        def body(x, carry):
            for c in range(CH):
                update(sec, x, c, None)
            return carry

        lax.fori_loop(1, NX - 1, body, 0)

    pack(0)
    pl.semaphore_wait(barrier, len(partners))
    start(tops_x)
    start(y_z_copies(0))
    for c in range(CH):
        start([x_copy(0, 0, c), x_copy(0, 1, c)])

    interior(0)
    top[2] = gather_top(1, tops_z, top_z)
    start(tops_y)
    value = gather_top(2, tops_y, top_y)
    value = jnp.max(jnp.max(value, axis=0, keepdims=True), axis=1, keepdims=True)
    step[...] = jnp.broadcast_to(COURANT * ELEM_WIDTH / (11.0 * value), (ROWS, NZ))
    loads[1].wait()

    for c in range(CH):
        for side in (0, 1):
            update_boundary(0, side, c)
            if c == 0:
                x_copy(1, side, c).start()
    update_interior(0)
    pack(1)
    start(y_z_copies(1))
    for c in range(1, CH):
        start([x_copy(1, 0, c), x_copy(1, 1, c)])

    interior(1)
    update_interior(1)
    for c in range(CH):
        for side in (0, 1):
            update_boundary(1, side, c)

    for copy in tops_x + tops_z + tops_y:
        copy.wait_send()
    for sec in (0, 1):
        for copy in y_z_copies(sec):
            copy.wait_send()
        for c in range(CH):
            for side in (0, 1):
                x_copy(sec, side, c).wait_send()


def shards(sizes, state, register):
    mat_z, mat_y = operators()
    nz, nxl, ny, nxh, nco = sizes
    n_x, n_z, n_y = nxh * nxl * nco - 1, nz - 1, ny - 1
    block = (NV, NX, NY, NZ)
    vmem = lambda *shape: pltpu.VMEM(shape, jnp.float32)
    dma = lambda *shape: pltpu.SemaphoreType.DMA(shape)
    out = jax.ShapeDtypeStruct(block, jnp.float32)
    return pl.pallas_call(
        functools.partial(kernel, sizes),
        out_shape=(out, out),
        in_specs=[pl.BlockSpec(memory_space=pl.ANY)] * 4,
        out_specs=[pl.BlockSpec(memory_space=pltpu.VMEM)] * 2,
        scratch_shapes=[
            vmem(*block),
            vmem(*block),
            vmem(*block),
            vmem(*block),
            vmem(*block),
            vmem(*block),
            vmem(2, 2 * LANES, 2 * LANES),
            vmem(NX * NY, NX * NY),
            vmem(ROWS, NZ),
            vmem(ROWS, NZ),
            vmem(3, ROWS, LANES),
            vmem(n_x, ROWS, LANES),
            vmem(n_z, ROWS, LANES),
            vmem(n_y, ROWS, LANES),
            vmem(2, 2, NV, ROWS, NZ),
            vmem(2, 2, NY, LANES),
            vmem(2, 2, NV, ROWS, NZ),
            vmem(2, 2, NY, LANES),
            vmem(2, 2, CH, NV, ROWS, NZ),
            vmem(2, NV, ROWS, NZ),
            vmem(2, NV, NY, LANES),
            dma(4),
            dma(2, 2, CH),
            dma(2, 2, CH),
            dma(2, 2, 2),
            dma(2, 2, 2),
            dma(n_x + n_z + n_y),
            dma(n_x + n_z + n_y),
        ],
        compiler_params=pltpu.CompilerParams(
            collective_id=0, has_side_effects=True, vmem_limit_bytes=40 * 2**20
        ),
        name="sections",
    )(state, register, mat_z, mat_y)


def solution(mesh):
    gx, gy, gz = (mesh.shape[a] for a in ("gx", "gy", "gz"))
    sizes = (gx // 2, 2, gy, gz // 2, 2)
    torus = Mesh(mesh.devices.reshape(sizes), AXES)
    placed = P(None, ("gx_0", "gx_1"), "gy", ("gz_0", "gz_1"))
    return jax.shard_map(
        functools.partial(shards, sizes),
        mesh=torus,
        in_specs=(placed, placed),
        out_specs=(placed, placed),
        check_vma=False,
    )
```

profile of v0, /device:TPU:1, one launch (start us, length us, event | category | flops | bytes accessed | tf_op | source)
XLA Modules:
  0.0 43.1 jit_solution(11664751265574123229)
XLA Ops:
  0.6 0.0 copy-start
  0.6 1.2 %copy-done = f32[5,6,24,384]{3,2,1,0:T(8,128)S(1)} copy-done((f32[5,6,24,384]{3,2,1,0:T(8,128)S(1)}, f32[5,6,24,384]{3,2,1,0:T(8,128)}, u32[]{:S(2)}) %copy-start) | copy-done | bytes 1105944
  1.9 0.0 copy-start.1
  1.9 1.2 %copy-done.1 = f32[5,6,24,384]{3,2,1,0:T(8,128)S(1)} copy-done((f32[5,6,24,384]{3,2,1,0:T(8,128)S(1)}, f32[5,6,24,384]{3,2,1,0:T(8,128)}, u32[]{:S(2)}) %copy-start.1) | copy-done | bytes 1105944
  3.1 0.0 copy-start.2
  3.1 1.0 %copy-done.2 = f32[2,256,256]{2,1,0:T(8,128)S(1)} copy-done((f32[2,256,256]{2,1,0:T(8,128)S(1)}, f32[2,256,256]{2,1,0:T(8,128)}, u32[]{:S(2)}) %copy-start.2) | copy-done | bytes 524312
  4.2 0.0 copy-start.3
  4.2 0.9 %copy-done.3 = f32[144,144]{1,0:T(8,128)S(1)} copy-done((f32[144,144]{1,0:T(8,128)S(1)}, f32[144,144]{1,0:T(8,128)}, u32[]{:S(2)}) %copy-start.3) | copy-done | bytes 82968
  5.1 36.0 %sections.1 = (f32[5,6,24,384]{3,2,1,0:T(8,128)S(1)}, f32[5,6,24,384]{3,2,1,0:T(8,128)S(1)}) custom-call(f32[5,6,24,384]{3,2,1,0:T(8,128)S(1)} %copy-done, f32[5,6,24,384]{3,2,1,0:T(8,128)S(1)} %copy-done.1, f32[2,256,256]{2,1,0:T(8,128)S(1)} %copy-done.2, f32[144,144]{1,0:T(8,128)S(1)} %copy-done.3), custom_call_target="tpu_custom_call" | custom-call | tf_op jit(solution)/shard_map/sections/pallas_call | solution.py:487
  41.1 1.0 %copy.8 = f32[5,6,24,384]{3,2,1,0:T(8,128)} copy(f32[5,6,24,384]{3,2,1,0:T(8,128)S(1)} %get-tuple-element.4) | data formatting | bytes 2211840
  42.1 1.0 %copy.9 = f32[5,6,24,384]{3,2,1,0:T(8,128)} copy(f32[5,6,24,384]{3,2,1,0:T(8,128)S(1)} %get-tuple-element.5) | data formatting | bytes 2211840
Async XLA Ops:
  0.6 1.2 %copy-start = (f32[5,6,24,384]{3,2,1,0:T(8,128)S(1)}, f32[5,6,24,384]{3,2,1,0:T(8,128)}, u32[]{:S(2)}) copy-start(f32[5,6,24,384]{3,2,1,0:T(8,128)} %state.1) | copy-start | bytes 3317764
  1.9 1.2 %copy-start.1 = (f32[5,6,24,384]{3,2,1,0:T(8,128)S(1)}, f32[5,6,24,384]{3,2,1,0:T(8,128)}, u32[]{:S(2)}) copy-start(f32[5,6,24,384]{3,2,1,0:T(8,128)} %register.1) | copy-start | bytes 3317764
  3.1 1.0 %copy-start.2 = (f32[2,256,256]{2,1,0:T(8,128)S(1)}, f32[2,256,256]{2,1,0:T(8,128)}, u32[]{:S(2)}) copy-start(f32[2,256,256]{2,1,0:T(8,128)} %constant.4.clone.mat_z) | copy-start | bytes 1572868
  4.2 0.9 %copy-start.3 = (f32[144,144]{1,0:T(8,128)S(1)}, f32[144,144]{1,0:T(8,128)}, u32[]{:S(2)}) copy-start(f32[144,144]{1,0:T(8,128)} %constant.5.clone.mat_y) | copy-start | bytes 248836
where the time goes:
time: 43.3 us; the launch traced here: 43.1 us
  Pallas kernels  36 us (83%)
  local copies, waits for them, and re-layouts  6.41 us (15%)
  between operations  0.65 us (2%)
    pallas_call x1, Pallas kernels, shards(): pl.pallas_call(functools.partial(kernel, sizes), out_shape=(out, out), in...  36 us
    unnamed x10, local copies, waits for them, and re-layouts  6.41 us

commit v1 on v0

--- a/solution.py
+++ b/solution.py
@@ -102,16 +102,28 @@
     return a, b
 
 
+def x_face(side, own, far):
+    a, b = face_terms(far, own, 0) if side == 0 else face_terms(own, far, 0)
+    return [p - q if side == 0 else p + q for p, q in zip(a, b)]
+
+
+def advance(sec, k, u, dt, r):
+    a, b = COEFFS[sec]
+    new_k = a * k + dt * r
+    return new_k, u + b * new_k
+
+
 def kernel(
     sizes,
     state,
     register,
     mat_z,
     mat_y,
-    out_state,
-    out_register,
     u,
     k,
+    edge,
+    far_x,
+    step,
     res,
     fx,
     fy,
@@ -119,7 +131,6 @@
     mz,
     my,
     mask_z,
-    step,
     top,
     top_x,
     top_z,
@@ -128,7 +139,7 @@
     z_pack,
     y_halo,
     z_halo,
-    x_halo,
+    near_x,
     y_corr,
     z_corr,
     load_sem,
@@ -242,7 +253,7 @@
         src = state if sec == 0 else u
         return remote(
             src.at[:, 0 if side == 0 else NX - 1, pl.ds(ROWS * c, ROWS), :],
-            x_halo.at[sec, 1 - side, c],
+            (far_x if sec else near_x).at[1 - side, c],
             send_x.at[sec, side, c],
             recv_x.at[sec, 1 - side, c],
             gx[side],
@@ -398,33 +409,23 @@
             loads[3].wait()
         lines_y_z()
         lines_x()
-        y_z_faces(sec)
 
     def update(sec, x, c, extra):
-        a, b = COEFFS[sec]
         rows = pl.ds(ROWS * c, ROWS)
-        dt = step[...]
         for v in range(NV):
             r = res[v, x, rows, :]
             if extra is not None:
                 r = r + extra[v]
-            new_k = a * k[v, x, rows, :] + dt * r
-            new_u = u[v, x, rows, :] + b * new_k
-            if sec == 0:
-                k[v, x, rows, :] = new_k
-                u[v, x, rows, :] = new_u
-            else:
-                out_register[v, x, rows, :] = new_k
-                out_state[v, x, rows, :] = new_u
-
-    def update_boundary(sec, side, c):
-        x_copy(sec, 1 - side, c).wait_recv()
+            new_k, new_u = advance(sec, k[v, x, rows, :], u[v, x, rows, :], step[...], r)
+            k[v, x, rows, :] = new_k
+            u[v, x, rows, :] = new_u
+
+    def update_boundary(side, c):
+        x_copy(0, 1 - side, c).wait_recv()
         x = 0 if side == 0 else NX - 1
         own = chunk(u, x, c)
-        far = [x_halo[sec, side, c, v] for v in range(NV)]
-        a, b = face_terms(far, own, 0) if side == 0 else face_terms(own, far, 0)
-        extra = [p - q if side == 0 else p + q for p, q in zip(a, b)]
-        update(sec, x, c, extra)
+        far = [near_x[side, c, v] for v in range(NV)]
+        update(0, x, c, x_face(side, own, far))
 
     def update_interior(sec):
         def body(x, carry):
@@ -434,9 +435,9 @@
 
         lax.fori_loop(1, NX - 1, body, 0)
 
-    pack(0)
     pl.semaphore_wait(barrier, len(partners))
     start(tops_x)
+    pack(0)
     start(y_z_copies(0))
     for c in range(CH):
         start([x_copy(0, 0, c), x_copy(0, 1, c)])
@@ -444,6 +445,7 @@
     interior(0)
     top[2] = gather_top(1, tops_z, top_z)
     start(tops_y)
+    y_z_faces(0)
     value = gather_top(2, tops_y, top_y)
     value = jnp.max(jnp.max(value, axis=0, keepdims=True), axis=1, keepdims=True)
     step[...] = jnp.broadcast_to(COURANT * ELEM_WIDTH / (11.0 * value), (ROWS, NZ))
@@ -451,7 +453,7 @@
 
     for c in range(CH):
         for side in (0, 1):
-            update_boundary(0, side, c)
+            update_boundary(side, c)
             if c == 0:
                 x_copy(1, side, c).start()
     update_interior(0)
@@ -461,10 +463,14 @@
         start([x_copy(1, 0, c), x_copy(1, 1, c)])
 
     interior(1)
+    y_z_faces(1)
     update_interior(1)
+    for v in range(NV):
+        edge[0, v] = res[v, 0]
+        edge[1, v] = res[v, NX - 1]
     for c in range(CH):
         for side in (0, 1):
-            update_boundary(1, side, c)
+            x_copy(1, side, c).wait_recv()
 
     for copy in tops_x + tops_z + tops_y:
         copy.wait_send()
@@ -476,6 +482,37 @@
                 x_copy(sec, side, c).wait_send()
 
 
+def finish(u, k, edge, far_x, step, out_state, out_register, done, sem):
+    inner = [
+        pltpu.make_async_copy(
+            src.at[:, pl.ds(1, NX - 2)], dst.at[:, pl.ds(1, NX - 2)], sem.at[i, 0]
+        )
+        for i, (src, dst) in enumerate(((u, out_state), (k, out_register)))
+    ]
+    for copy in inner:
+        copy.start()
+    outer = []
+    for side in (0, 1):
+        x = 0 if side == 0 else NX - 1
+        for c in range(CH):
+            rows = pl.ds(ROWS * c, ROWS)
+            own = [u[v, x, rows, :] for v in range(NV)]
+            far = [far_x[side, c, v] for v in range(NV)]
+            extra = x_face(side, own, far)
+            for v in range(NV):
+                new_k, new_u = advance(
+                    1, k[v, x, rows, :], own[v], step[...], edge[side, v, rows, :] + extra[v]
+                )
+                done[0, side, v, rows, :] = new_u
+                done[1, side, v, rows, :] = new_k
+        for i, dst in enumerate((out_state, out_register)):
+            copy = pltpu.make_async_copy(done.at[i, side], dst.at[:, x], sem.at[i, 1 + side])
+            copy.start()
+            outer.append(copy)
+    for copy in inner + outer:
+        copy.wait()
+
+
 def shards(sizes, state, register):
     mat_z, mat_y = operators()
     nz, nxl, ny, nxh, nco = sizes
@@ -483,22 +520,27 @@
     block = (NV, NX, NY, NZ)
     vmem = lambda *shape: pltpu.VMEM(shape, jnp.float32)
     dma = lambda *shape: pltpu.SemaphoreType.DMA(shape)
-    out = jax.ShapeDtypeStruct(block, jnp.float32)
-    return pl.pallas_call(
+    array = lambda *shape: jax.ShapeDtypeStruct(shape, jnp.float32)
+    in_vmem = pl.BlockSpec(memory_space=pltpu.VMEM)
+    in_hbm = pl.BlockSpec(memory_space=pltpu.HBM)
+    parts = pl.pallas_call(
         functools.partial(kernel, sizes),
-        out_shape=(out, out),
-        in_specs=[pl.BlockSpec(memory_space=pl.ANY)] * 4,
-        out_specs=[pl.BlockSpec(memory_space=pltpu.VMEM)] * 2,
+        out_shape=(
+            array(*block),
+            array(*block),
+            array(2, NV, NY, NZ),
+            array(2, CH, NV, ROWS, NZ),
+            array(ROWS, NZ),
+        ),
+        in_specs=[in_hbm] * 4,
+        out_specs=[in_vmem] * 5,
         scratch_shapes=[
-            vmem(*block),
-            vmem(*block),
             vmem(*block),
             vmem(*block),
             vmem(*block),
             vmem(*block),
             vmem(2, 2 * LANES, 2 * LANES),
             vmem(NX * NY, NX * NY),
-            vmem(ROWS, NZ),
             vmem(ROWS, NZ),
             vmem(3, ROWS, LANES),
             vmem(n_x, ROWS, LANES),
@@ -508,7 +550,7 @@
             vmem(2, 2, NY, LANES),
             vmem(2, 2, NV, ROWS, NZ),
             vmem(2, 2, NY, LANES),
-            vmem(2, 2, CH, NV, ROWS, NZ),
+            vmem(2, CH, NV, ROWS, NZ),
             vmem(2, NV, ROWS, NZ),
             vmem(2, NV, NY, LANES),
             dma(4),
@@ -520,10 +562,19 @@
             dma(n_x + n_z + n_y),
         ],
         compiler_params=pltpu.CompilerParams(
-            collective_id=0, has_side_effects=True, vmem_limit_bytes=40 * 2**20
+            collective_id=0, has_side_effects=True, vmem_limit_bytes=32 * 2**20
         ),
         name="sections",
-    )(state, register, mat_z, mat_y)
+    )(*[pltpu.with_memory_space_constraint(x, pltpu.HBM) for x in (state, register, mat_z, mat_y)])
+    return pl.pallas_call(
+        finish,
+        out_shape=(array(*block), array(*block)),
+        in_specs=[in_vmem] * 5,
+        out_specs=[in_hbm] * 2,
+        scratch_shapes=[vmem(2, 2, NV, NY, NZ), dma(2, 3)],
+        compiler_params=pltpu.CompilerParams(vmem_limit_bytes=16 * 2**20),
+        name="finish",
+    )(*parts)
 
 
 def solution(mesh):

time: 43.3 us -> 37.4 us (0.86)
  local copies, waits for them, and re-layouts: 6.41 us -> 0 us
  Pallas kernels: 36 us -> 36.7 us
    unnamed x10 -> x0, local copies, waits for them, and re-layouts: 6.41 us -> none
    pallas_call x1 -> x2, Pallas kernels: 36 us -> 36.7 us  [the longest x1 35.3 us: shards(): pl.pallas_call(functools.partial(kernel, sizes), out_shape=(array(*block)...]
where the time goes in v1:
time: 37.4 us; the launch traced here: 37.3 us
  Pallas kernels  36.7 us (98%)
  between operations  0.64 us (2%)
    pallas_call x1, Pallas kernels, shards(): pl.pallas_call(functools.partial(kernel, sizes), out_shape=(array(*block)...  35.3 us
    pallas_call x1, Pallas kernels, shards(): pl.pallas_call(finish, out_shape=(array(*block), array(*block)), in_specs...  1.4 us

profile of v1, /device:TPU:1, one launch (start us, length us, event | category | flops | bytes accessed | tf_op | source)
XLA Modules:
  0.0 37.3 jit_solution(6889034725162184774)
XLA Ops:
  0.6 35.3 %sections.1 = (f32[5,6,24,384]{3,2,1,0:T(8,128)S(1)}, f32[5,6,24,384]{3,2,1,0:T(8,128)S(1)}, f32[2,5,24,384]{3,2,1,0:T(8,128)S(1)}, f32[2,3,5,8,384]{4,3,2,1,0:T(8,128)S(1)}, f32[8,384]{1,0:T(8,128)S(1)}) custom-call(f32[5,6,24,384]{3,2,1,0:T(8,128)} %state.1, f32[5,6,24,384]{3,2,1,0:T(8,128)} %register.1, f32[2,256,256]{2,1,0:T(8,128)} %constant.4.clone.mat_z, ...), custom_call_target="tpu_custom_call" | custom-call | tf_op jit(solution)/shard_map/sections/pallas_call | solution.py:526
  35.9 1.4 %finish.1 = (f32[5,6,24,384]{3,2,1,0:T(8,128)}, f32[5,6,24,384]{3,2,1,0:T(8,128)}) custom-call(f32[5,6,24,384]{3,2,1,0:T(8,128)S(1)} %get-tuple-element.7.u, f32[5,6,24,384]{3,2,1,0:T(8,128)S(1)} %get-tuple-element.8.k, f32[2,5,24,384]{3,2,1,0:T(8,128)S(1)} %get-tuple-element.9.edge, f32[2,3,5,8,384]{4,3,2,1,0:T(8,128)S(1)} %get-tuple-element.10.far_x, ...), custom_call_target="tpu_custom_call" | custom-call | tf_op jit(solution)/shard_map/finish/pallas_call | solution.py:569

commit v2 on v1

--- a/solution.py
+++ b/solution.py
@@ -132,9 +132,8 @@
     my,
     mask_z,
     top,
-    top_x,
-    top_z,
-    top_y,
+    top_far,
+    top_near,
     y_pack,
     z_pack,
     y_halo,
@@ -169,27 +168,40 @@
         device(xh_=wrap(xh + co - 1, nxh), co_=other_co),
         device(xh_=wrap(xh + co, nxh), co_=other_co),
     )
-    group_x = [
-        device(xh_=wrap(xh + a, nxh), xl_=wrap(xl + b, nxl), co_=wrap(co + c, nco))
+    far = [
+        (min(i, nz - i) + (2 * a if a != b else 1 if b else 0), i, a, b)
+        for i in range(nz)
         for a in range(nxh)
         for b in range(nxl)
+        if i or a or b
+    ]
+    group_far = [
+        device(z_=wrap(z + i, nz), xh_=wrap(xh + a, nxh), xl_=wrap(xl + b, nxl))
+        for _, i, a, b in sorted(far, reverse=True)
+    ]
+    group_near = [
+        device(y_=wrap(y + i, ny), co_=wrap(co + c, nco))
+        for i in range(ny)
         for c in range(nco)
-        if a or b or c
+        if i or c
     ]
-    group_z = [device(z_=wrap(z + i, nz)) for i in range(1, nz)]
-    group_y = [device(y_=wrap(y + i, ny)) for i in range(1, ny)]
-    diagonal = device(z_=wrap(z + 2 * xl - 1, nz), xl_=other_xl)
+    across = [device(xh_=wrap(xh + 1, nxh), co_=other_co)]
 
     loads = [
-        pltpu.make_async_copy(state, u, load_sem.at[0]),
-        pltpu.make_async_copy(register, k, load_sem.at[1]),
-        pltpu.make_async_copy(mat_z, mz, load_sem.at[2]),
-        pltpu.make_async_copy(mat_y, my, load_sem.at[3]),
+        pltpu.make_async_copy(mat_z, mz, load_sem.at[NX]),
+        pltpu.make_async_copy(mat_y, my, load_sem.at[NX + 1]),
+        pltpu.make_async_copy(register, k, load_sem.at[NX + 2]),
     ]
+
+    def load_plane(x):
+        return pltpu.make_async_copy(state.at[:, x], u.at[:, x], load_sem.at[x])
+
+    for x in range(NX):
+        load_plane(x).start()
     for load in loads:
         load.start()
     barrier = pltpu.get_barrier_semaphore()
-    partners = group_x + group_z + group_y + [diagonal]
+    partners = group_far + group_near + across[: nxh - 1]
     for partner in partners:
         pl.semaphore_signal(barrier, inc=1, device_id=partner, device_id_type=MESH)
 
@@ -203,10 +215,8 @@
     def chunk(ref, x, c):
         return [ref[v, x, pl.ds(ROWS * c, ROWS), :] for v in range(NV)]
 
-    loads[0].wait()
-    top[0] = jnp.zeros((ROWS, LANES), jnp.float32)
-
     def speed_body(x, carry):
+        load_plane(x).wait()
         for c in range(CH):
             w = chunk(u, x, c)
             vel, press, sound = primitives(w)
@@ -216,9 +226,10 @@
         return carry
 
     best = lax.fori_loop(0, NX, speed_body, jnp.zeros((ROWS, NZ), jnp.float32))
-    top[0] = jnp.maximum(
+    best = jnp.maximum(
         jnp.maximum(best[:, :LANES], best[:, LANES : 2 * LANES]), best[:, 2 * LANES :]
     )
+    top[0] = jnp.max(best, axis=0, keepdims=True)
 
     def pack(sec):
         def body(v, carry):
@@ -283,9 +294,8 @@
             for i, to in enumerate(group)
         ]
 
-    tops_x = top_copies(0, group_x, top_x, 0)
-    tops_z = top_copies(1, group_z, top_z, len(group_x))
-    tops_y = top_copies(2, group_y, top_y, len(group_x) + len(group_z))
+    tops_far = top_copies(0, group_far, top_far, 0)
+    tops_near = top_copies(1, group_near, top_near, len(group_far))
 
     def start(copies):
         for copy in copies:
@@ -402,11 +412,10 @@
     def interior(sec):
         fluxes_and_jumps()
         if sec == 0:
-            value = gather_top(0, tops_x, top_x)
-            top[1] = value
-            start(tops_z)
-            loads[2].wait()
-            loads[3].wait()
+            loads[0].wait()
+            loads[1].wait()
+            top[1] = gather_top(0, tops_far, top_far)
+            start(tops_near)
         lines_y_z()
         lines_x()
 
@@ -436,31 +445,29 @@
         lax.fori_loop(1, NX - 1, body, 0)
 
     pl.semaphore_wait(barrier, len(partners))
-    start(tops_x)
+    start(tops_far)
+    start([x_copy(0, 0, 0), x_copy(0, 1, 0)])
     pack(0)
     start(y_z_copies(0))
-    for c in range(CH):
+    for c in range(1, CH):
         start([x_copy(0, 0, c), x_copy(0, 1, c)])
 
     interior(0)
-    top[2] = gather_top(1, tops_z, top_z)
-    start(tops_y)
     y_z_faces(0)
-    value = gather_top(2, tops_y, top_y)
-    value = jnp.max(jnp.max(value, axis=0, keepdims=True), axis=1, keepdims=True)
+    value = gather_top(1, tops_near, top_near)
+    value = jnp.max(jnp.broadcast_to(value, (ROWS, LANES)), axis=1, keepdims=True)
     step[...] = jnp.broadcast_to(COURANT * ELEM_WIDTH / (11.0 * value), (ROWS, NZ))
-    loads[1].wait()
+    loads[2].wait()
 
     for c in range(CH):
         for side in (0, 1):
             update_boundary(side, c)
-            if c == 0:
+            if c < CH - 1:
                 x_copy(1, side, c).start()
     update_interior(0)
     pack(1)
     start(y_z_copies(1))
-    for c in range(1, CH):
-        start([x_copy(1, 0, c), x_copy(1, 1, c)])
+    start([x_copy(1, 0, CH - 1), x_copy(1, 1, CH - 1)])
 
     interior(1)
     y_z_faces(1)
@@ -472,7 +479,7 @@
         for side in (0, 1):
             x_copy(1, side, c).wait_recv()
 
-    for copy in tops_x + tops_z + tops_y:
+    for copy in tops_far + tops_near:
         copy.wait_send()
     for sec in (0, 1):
         for copy in y_z_copies(sec):
@@ -516,7 +523,7 @@
 def shards(sizes, state, register):
     mat_z, mat_y = operators()
     nz, nxl, ny, nxh, nco = sizes
-    n_x, n_z, n_y = nxh * nxl * nco - 1, nz - 1, ny - 1
+    n_far, n_near = nz * nxh * nxl - 1, ny * nco - 1
     block = (NV, NX, NY, NZ)
     vmem = lambda *shape: pltpu.VMEM(shape, jnp.float32)
     dma = lambda *shape: pltpu.SemaphoreType.DMA(shape)
@@ -542,10 +549,9 @@
             vmem(2, 2 * LANES, 2 * LANES),
             vmem(NX * NY, NX * NY),
             vmem(ROWS, NZ),
-            vmem(3, ROWS, LANES),
-            vmem(n_x, ROWS, LANES),
-            vmem(n_z, ROWS, LANES),
-            vmem(n_y, ROWS, LANES),
+            vmem(2, 1, LANES),
+            vmem(n_far, 1, LANES),
+            vmem(n_near, 1, LANES),
             vmem(2, 2, NV, ROWS, NZ),
             vmem(2, 2, NY, LANES),
             vmem(2, 2, NV, ROWS, NZ),
@@ -553,13 +559,13 @@
             vmem(2, CH, NV, ROWS, NZ),
             vmem(2, NV, ROWS, NZ),
             vmem(2, NV, NY, LANES),
-            dma(4),
+            dma(NX + 3),
             dma(2, 2, CH),
             dma(2, 2, CH),
             dma(2, 2, 2),
             dma(2, 2, 2),
-            dma(n_x + n_z + n_y),
-            dma(n_x + n_z + n_y),
+            dma(n_far + n_near),
+            dma(n_far + n_near),
         ],
         compiler_params=pltpu.CompilerParams(
             collective_id=0, has_side_effects=True, vmem_limit_bytes=32 * 2**20

time: 37.4 us -> 34.7 us (0.928)
  Pallas kernels: 36.7 us -> 34 us
    pallas_call x1, Pallas kernels: 35.3 us -> 32.6 us  [shards(): pl.pallas_call(functools.partial(kernel, sizes), out_shape=(array(*block)...]
where the time goes in v2:
time: 34.7 us; the launch traced here: 34.6 us
  Pallas kernels  34 us (98%)
  between operations  0.64 us (2%)
    pallas_call x1, Pallas kernels, shards(): pl.pallas_call(functools.partial(kernel, sizes), out_shape=(array(*block)...  32.6 us
    pallas_call x1, Pallas kernels, shards(): pl.pallas_call(finish, out_shape=(array(*block), array(*block)), in_specs...  1.4 us

profile of v2, /device:TPU:1, one launch (start us, length us, event | category | flops | bytes accessed | tf_op | source)
XLA Modules:
  0.0 34.6 jit_solution(1412312443616745986)
XLA Ops:
  0.6 32.6 %sections.1 = (f32[5,6,24,384]{3,2,1,0:T(8,128)S(1)}, f32[5,6,24,384]{3,2,1,0:T(8,128)S(1)}, f32[2,5,24,384]{3,2,1,0:T(8,128)S(1)}, f32[2,3,5,8,384]{4,3,2,1,0:T(8,128)S(1)}, f32[8,384]{1,0:T(8,128)S(1)}) custom-call(f32[5,6,24,384]{3,2,1,0:T(8,128)} %state.1, f32[5,6,24,384]{3,2,1,0:T(8,128)} %register.1, f32[2,256,256]{2,1,0:T(8,128)} %constant.4.clone.mat_z, ...), custom_call_target="tpu_custom_call" | custom-call | tf_op jit(solution)/shard_map/sections/pallas_call | solution.py:533
  33.2 1.4 %finish.1 = (f32[5,6,24,384]{3,2,1,0:T(8,128)}, f32[5,6,24,384]{3,2,1,0:T(8,128)}) custom-call(f32[5,6,24,384]{3,2,1,0:T(8,128)S(1)} %get-tuple-element.7.u, f32[5,6,24,384]{3,2,1,0:T(8,128)S(1)} %get-tuple-element.8.k, f32[2,5,24,384]{3,2,1,0:T(8,128)S(1)} %get-tuple-element.9.edge, f32[2,3,5,8,384]{4,3,2,1,0:T(8,128)S(1)} %get-tuple-element.10.far_x, ...), custom_call_target="tpu_custom_call" | custom-call | tf_op jit(solution)/shard_map/finish/pallas_call | solution.py:575

commit v3 on v2

--- a/solution.py
+++ b/solution.py
@@ -74,6 +74,14 @@
     return (
         jnp.asarray(np.stack([low, high]), jnp.float32),
         jnp.asarray(along_y, jnp.float32),
+    )
+
+
+def z_steps(nz):
+    assert nz <= 8
+    return (
+        sorted({i % nz for i in (1, -1, 2, -2)} - {0}),
+        sorted({i % nz for i in (0, 2, -2)}),
     )
 
 
@@ -132,8 +140,9 @@
     my,
     mask_z,
     top,
-    top_far,
-    top_near,
+    top_1,
+    top_2,
+    top_3,
     y_pack,
     z_pack,
     y_halo,
@@ -168,24 +177,26 @@
         device(xh_=wrap(xh + co - 1, nxh), co_=other_co),
         device(xh_=wrap(xh + co, nxh), co_=other_co),
     )
-    far = [
-        (min(i, nz - i) + (2 * a if a != b else 1 if b else 0), i, a, b)
-        for i in range(nz)
+    def at(i, a, b, c):
+        return device(
+            z_=wrap(z + i, nz), xh_=wrap(xh + a, nxh), xl_=wrap(xl + b, nxl), co_=wrap(co + c, nco)
+        )
+
+    steps_1, steps_2 = z_steps(nz)
+    group_1 = [device(z_=wrap(z + i, nz)) for i in steps_1]
+    group_2 = [
+        at(i, a, b, c)
+        for i in steps_2
         for a in range(nxh)
         for b in range(nxl)
-        if i or a or b
+        for c in range(nco)
+        if i or a or b or c
     ]
-    group_far = [
-        device(z_=wrap(z + i, nz), xh_=wrap(xh + a, nxh), xl_=wrap(xl + b, nxl))
-        for _, i, a, b in sorted(far, reverse=True)
+    group_3 = [device(y_=wrap(y + i, ny)) for i in range(1, ny)]
+    group_x = [
+        at(0, a, b, c) for a in range(nxh) for b in range(nxl) for c in range(nco) if a or b or c
     ]
-    group_near = [
-        device(y_=wrap(y + i, ny), co_=wrap(co + c, nco))
-        for i in range(ny)
-        for c in range(nco)
-        if i or c
-    ]
-    across = [device(xh_=wrap(xh + 1, nxh), co_=other_co)]
+    diagonal = device(z_=wrap(z + 2 * xl - 1, nz), xl_=other_xl)
 
     loads = [
         pltpu.make_async_copy(mat_z, mz, load_sem.at[NX]),
@@ -201,7 +212,7 @@
     for load in loads:
         load.start()
     barrier = pltpu.get_barrier_semaphore()
-    partners = group_far + group_near + across[: nxh - 1]
+    partners = group_1 + group_x + group_3 + [diagonal]
     for partner in partners:
         pl.semaphore_signal(barrier, inc=1, device_id=partner, device_id_type=MESH)
 
@@ -294,8 +305,9 @@
             for i, to in enumerate(group)
         ]
 
-    tops_far = top_copies(0, group_far, top_far, 0)
-    tops_near = top_copies(1, group_near, top_near, len(group_far))
+    tops_1 = top_copies(0, group_1, top_1, 0)
+    tops_2 = top_copies(1, group_2, top_2, len(group_1))
+    tops_3 = top_copies(2, group_3, top_3, len(group_1) + len(group_2))
 
     def start(copies):
         for copy in copies:
@@ -409,16 +421,6 @@
 
         lax.fori_loop(0, NV, body, 0)
 
-    def interior(sec):
-        fluxes_and_jumps()
-        if sec == 0:
-            loads[0].wait()
-            loads[1].wait()
-            top[1] = gather_top(0, tops_far, top_far)
-            start(tops_near)
-        lines_y_z()
-        lines_x()
-
     def update(sec, x, c, extra):
         rows = pl.ds(ROWS * c, ROWS)
         for v in range(NV):
@@ -445,16 +447,23 @@
         lax.fori_loop(1, NX - 1, body, 0)
 
     pl.semaphore_wait(barrier, len(partners))
-    start(tops_far)
+    start(tops_1)
     start([x_copy(0, 0, 0), x_copy(0, 1, 0)])
     pack(0)
     start(y_z_copies(0))
+    fluxes_and_jumps()
+    top[1] = gather_top(0, tops_1, top_1)
+    start(tops_2)
     for c in range(1, CH):
         start([x_copy(0, 0, c), x_copy(0, 1, c)])
-
-    interior(0)
+    loads[0].wait()
+    loads[1].wait()
+    lines_y_z()
+    top[2] = gather_top(1, tops_2, top_2)
+    start(tops_3)
+    lines_x()
     y_z_faces(0)
-    value = gather_top(1, tops_near, top_near)
+    value = gather_top(2, tops_3, top_3)
     value = jnp.max(jnp.broadcast_to(value, (ROWS, LANES)), axis=1, keepdims=True)
     step[...] = jnp.broadcast_to(COURANT * ELEM_WIDTH / (11.0 * value), (ROWS, NZ))
     loads[2].wait()
@@ -469,7 +478,9 @@
     start(y_z_copies(1))
     start([x_copy(1, 0, CH - 1), x_copy(1, 1, CH - 1)])
 
-    interior(1)
+    fluxes_and_jumps()
+    lines_y_z()
+    lines_x()
     y_z_faces(1)
     update_interior(1)
     for v in range(NV):
@@ -479,7 +490,7 @@
         for side in (0, 1):
             x_copy(1, side, c).wait_recv()
 
-    for copy in tops_far + tops_near:
+    for copy in tops_1 + tops_2 + tops_3:
         copy.wait_send()
     for sec in (0, 1):
         for copy in y_z_copies(sec):
@@ -523,7 +534,8 @@
 def shards(sizes, state, register):
     mat_z, mat_y = operators()
     nz, nxl, ny, nxh, nco = sizes
-    n_far, n_near = nz * nxh * nxl - 1, ny * nco - 1
+    steps_1, steps_2 = z_steps(nz)
+    counts = (len(steps_1), len(steps_2) * nxh * nxl * nco - 1, ny - 1)
     block = (NV, NX, NY, NZ)
     vmem = lambda *shape: pltpu.VMEM(shape, jnp.float32)
     dma = lambda *shape: pltpu.SemaphoreType.DMA(shape)
@@ -549,9 +561,10 @@
             vmem(2, 2 * LANES, 2 * LANES),
             vmem(NX * NY, NX * NY),
             vmem(ROWS, NZ),
-            vmem(2, 1, LANES),
-            vmem(n_far, 1, LANES),
-            vmem(n_near, 1, LANES),
+            vmem(3, 1, LANES),
+            vmem(counts[0], 1, LANES),
+            vmem(counts[1], 1, LANES),
+            vmem(counts[2], 1, LANES),
             vmem(2, 2, NV, ROWS, NZ),
             vmem(2, 2, NY, LANES),
             vmem(2, 2, NV, ROWS, NZ),
@@ -564,8 +577,8 @@
             dma(2, 2, CH),
             dma(2, 2, 2),
             dma(2, 2, 2),
-            dma(n_far + n_near),
-            dma(n_far + n_near),
+            dma(sum(counts)),
+            dma(sum(counts)),
         ],
         compiler_params=pltpu.CompilerParams(
             collective_id=0, has_side_effects=True, vmem_limit_bytes=32 * 2**20

time: 34.7 us -> 35.4 us (1.020)
  Pallas kernels: 34 us -> 34.7 us
    pallas_call x1, Pallas kernels: 32.6 us -> 33.3 us  [shards(): pl.pallas_call(functools.partial(kernel, sizes), out_shape=(array(*block)...]
where the time goes in v3:
time: 35.4 us; the launch traced here: 35.3 us
  Pallas kernels  34.7 us (98%)
  between operations  0.64 us (2%)
    pallas_call x1, Pallas kernels, shards(): pl.pallas_call(functools.partial(kernel, sizes), out_shape=(array(*block)...  33.3 us
    pallas_call x1, Pallas kernels, shards(): pl.pallas_call(finish, out_shape=(array(*block), array(*block)), in_specs...  1.4 us

profile of v3, /device:TPU:1, one launch (start us, length us, event | category | flops | bytes accessed | tf_op | source)
XLA Modules:
  0.0 35.3 jit_solution(1838699761264681360)
XLA Ops:
  0.6 33.3 %sections.1 = (f32[5,6,24,384]{3,2,1,0:T(8,128)S(1)}, f32[5,6,24,384]{3,2,1,0:T(8,128)S(1)}, f32[2,5,24,384]{3,2,1,0:T(8,128)S(1)}, f32[2,3,5,8,384]{4,3,2,1,0:T(8,128)S(1)}, f32[8,384]{1,0:T(8,128)S(1)}) custom-call(f32[5,6,24,384]{3,2,1,0:T(8,128)} %state.1, f32[5,6,24,384]{3,2,1,0:T(8,128)} %register.1, f32[2,256,256]{2,1,0:T(8,128)} %constant.4.clone.mat_z, ...), custom_call_target="tpu_custom_call" | custom-call | tf_op jit(solution)/shard_map/sections/pallas_call | solution.py:545
  33.9 1.4 %finish.1 = (f32[5,6,24,384]{3,2,1,0:T(8,128)}, f32[5,6,24,384]{3,2,1,0:T(8,128)}) custom-call(f32[5,6,24,384]{3,2,1,0:T(8,128)S(1)} %get-tuple-element.7.u, f32[5,6,24,384]{3,2,1,0:T(8,128)S(1)} %get-tuple-element.8.k, f32[2,5,24,384]{3,2,1,0:T(8,128)S(1)} %get-tuple-element.9.edge, f32[2,3,5,8,384]{4,3,2,1,0:T(8,128)S(1)} %get-tuple-element.10.far_x, ...), custom_call_target="tpu_custom_call" | custom-call | tf_op jit(solution)/shard_map/finish/pallas_call | solution.py:588

commit v4 on v3

--- a/solution.py
+++ b/solution.py
@@ -63,6 +63,11 @@
     return op
 
 
+def halves(x):
+    top = x.astype(jnp.bfloat16)
+    return top, (x - top.astype(jnp.float32)).astype(jnp.bfloat16)
+
+
 def operators():
     along_z = line_operator(NZ).T
     cut = 2 * LANES - (2 * LANES) % N
@@ -71,10 +76,7 @@
     high = along_z[LANES:, LANES:].copy()
     high[:, : cut - LANES] = 0.0
     along_y = np.kron(np.eye(NX), line_operator(NY))
-    return (
-        jnp.asarray(np.stack([low, high]), jnp.float32),
-        jnp.asarray(along_y, jnp.float32),
-    )
+    return tuple(jnp.stack(halves(jnp.asarray(m, jnp.float32))) for m in (np.stack([low, high]), along_y))
 
 
 def z_steps(nz):
@@ -131,6 +133,7 @@
     k,
     edge,
     far_x,
+    far_ab,
     step,
     res,
     fx,
@@ -148,11 +151,14 @@
     y_halo,
     z_halo,
     near_x,
+    ab,
     y_corr,
     z_corr,
     load_sem,
     send_x,
     recv_x,
+    send_ab,
+    recv_ab,
     send_yz,
     recv_yz,
     send_top,
@@ -275,9 +281,18 @@
         src = state if sec == 0 else u
         return remote(
             src.at[:, 0 if side == 0 else NX - 1, pl.ds(ROWS * c, ROWS), :],
-            (far_x if sec else near_x).at[1 - side, c],
+            far_x.at[1 - side, c - 1] if sec else near_x.at[1 - side, c],
             send_x.at[sec, side, c],
             recv_x.at[sec, 1 - side, c],
+            gx[side],
+        )
+
+    def ab_copy(part, side):
+        return remote(
+            ab.at[part, side],
+            far_ab.at[part, 1 - side],
+            send_ab.at[part, side],
+            recv_ab.at[part, 1 - side],
             gx[side],
         )
 
@@ -351,19 +366,19 @@
         lax.fori_loop(0, NX, body, 0)
 
     def dot(a, b):
-        return jnp.dot(
-            a, b, precision=lax.Precision.HIGHEST, preferred_element_type=jnp.float32
-        )
+        (a_top, a_rest), (b_top, b_rest) = a, b
+        one = lambda p, q: jnp.dot(p, q, preferred_element_type=jnp.float32)
+        return one(a_top, b_top) + (one(a_top, b_rest) + one(a_rest, b_top))
 
     def lines_y_z():
         def body(v, carry):
-            along_z = fz[v].reshape(NX * NY, NZ)
-            low = dot(along_z[:, : 2 * LANES], mz[0])
-            high = dot(along_z[:, LANES:], mz[1])
+            along_z = halves(fz[v].reshape(NX * NY, NZ))
+            low = dot([p[:, : 2 * LANES] for p in along_z], (mz[0, 0], mz[1, 0]))
+            high = dot([p[:, LANES:] for p in along_z], (mz[0, 1], mz[1, 1]))
             both = jnp.concatenate(
                 [low[:, :LANES], low[:, LANES:] + high[:, :LANES], high[:, LANES:]], axis=1
             )
-            along_y = dot(my[...], fy[v].reshape(NX * NY, NZ))
+            along_y = dot((my[0], my[1]), halves(fy[v].reshape(NX * NY, NZ)))
             res[v] = res[v] + (both + along_y).reshape(NX, NY, NZ)
             return carry
 
@@ -431,12 +446,27 @@
             k[v, x, rows, :] = new_k
             u[v, x, rows, :] = new_u
 
-    def update_boundary(side, c):
+    def plane(side):
+        return 0 if side == 0 else NX - 1
+
+    def known_part(side):
+        a, b = COEFFS[0]
+        rows = pl.ds(0, ROWS)
+        for v in range(NV):
+            ab[0, side, v] = u[v, plane(side), rows, :] + b * (a * k[v, plane(side), rows, :])
+        ab_copy(0, side).start()
+
+    def step_part(side):
+        extra = boundary_terms(side, 0)
+        for v in range(NV):
+            r = res[v, plane(side), 0:ROWS, :] + extra[v]
+            res[v, plane(side), 0:ROWS, :] = r
+            ab[1, side, v] = COEFFS[0][1] * r
+        ab_copy(1, side).start()
+
+    def boundary_terms(side, c):
         x_copy(0, 1 - side, c).wait_recv()
-        x = 0 if side == 0 else NX - 1
-        own = chunk(u, x, c)
-        far = [near_x[side, c, v] for v in range(NV)]
-        update(0, x, c, x_face(side, own, far))
+        return x_face(side, chunk(u, plane(side), c), [near_x[side, c, v] for v in range(NV)])
 
     def update_interior(sec):
         def body(x, carry):
@@ -456,6 +486,9 @@
     start(tops_2)
     for c in range(1, CH):
         start([x_copy(0, 0, c), x_copy(0, 1, c)])
+    loads[2].wait()
+    for side in (0, 1):
+        known_part(side)
     loads[0].wait()
     loads[1].wait()
     lines_y_z()
@@ -463,15 +496,16 @@
     start(tops_3)
     lines_x()
     y_z_faces(0)
+    for side in (0, 1):
+        step_part(side)
     value = gather_top(2, tops_3, top_3)
     value = jnp.max(jnp.broadcast_to(value, (ROWS, LANES)), axis=1, keepdims=True)
     step[...] = jnp.broadcast_to(COURANT * ELEM_WIDTH / (11.0 * value), (ROWS, NZ))
-    loads[2].wait()
-
-    for c in range(CH):
+
+    for c in (*range(1, CH), 0):
         for side in (0, 1):
-            update_boundary(side, c)
-            if c < CH - 1:
+            update(0, plane(side), c, boundary_terms(side, c) if c else None)
+            if 0 < c < CH - 1:
                 x_copy(1, side, c).start()
     update_interior(0)
     pack(1)
@@ -486,8 +520,10 @@
     for v in range(NV):
         edge[0, v] = res[v, 0]
         edge[1, v] = res[v, NX - 1]
-    for c in range(CH):
-        for side in (0, 1):
+    for side in (0, 1):
+        for part in (0, 1):
+            ab_copy(part, side).wait_recv()
+        for c in range(1, CH):
             x_copy(1, side, c).wait_recv()
 
     for copy in tops_1 + tops_2 + tops_3:
@@ -495,12 +531,13 @@
     for sec in (0, 1):
         for copy in y_z_copies(sec):
             copy.wait_send()
-        for c in range(CH):
-            for side in (0, 1):
+        for side in (0, 1):
+            ab_copy(sec, side).wait_send()
+            for c in range(sec, CH):
                 x_copy(sec, side, c).wait_send()
 
 
-def finish(u, k, edge, far_x, step, out_state, out_register, done, sem):
+def finish(u, k, edge, far_x, far_ab, step, out_state, out_register, done, sem):
     inner = [
         pltpu.make_async_copy(
             src.at[:, pl.ds(1, NX - 2)], dst.at[:, pl.ds(1, NX - 2)], sem.at[i, 0]
@@ -515,7 +552,10 @@
         for c in range(CH):
             rows = pl.ds(ROWS * c, ROWS)
             own = [u[v, x, rows, :] for v in range(NV)]
-            far = [far_x[side, c, v] for v in range(NV)]
+            if c:
+                far = [far_x[side, c - 1, v] for v in range(NV)]
+            else:
+                far = [far_ab[0, side, v] + step[...] * far_ab[1, side, v] for v in range(NV)]
             extra = x_face(side, own, far)
             for v in range(NV):
                 new_k, new_u = advance(
@@ -548,18 +588,19 @@
             array(*block),
             array(*block),
             array(2, NV, NY, NZ),
-            array(2, CH, NV, ROWS, NZ),
+            array(2, CH - 1, NV, ROWS, NZ),
+            array(2, 2, NV, ROWS, NZ),
             array(ROWS, NZ),
         ),
         in_specs=[in_hbm] * 4,
-        out_specs=[in_vmem] * 5,
+        out_specs=[in_vmem] * 6,
         scratch_shapes=[
             vmem(*block),
             vmem(*block),
             vmem(*block),
             vmem(*block),
-            vmem(2, 2 * LANES, 2 * LANES),
-            vmem(NX * NY, NX * NY),
+            pltpu.VMEM((2, 2, 2 * LANES, 2 * LANES), jnp.bfloat16),
+            pltpu.VMEM((2, NX * NY, NX * NY), jnp.bfloat16),
             vmem(ROWS, NZ),
             vmem(3, 1, LANES),
             vmem(counts[0], 1, LANES),
@@ -570,11 +611,14 @@
             vmem(2, 2, NV, ROWS, NZ),
             vmem(2, 2, NY, LANES),
             vmem(2, CH, NV, ROWS, NZ),
+            vmem(2, 2, NV, ROWS, NZ),
             vmem(2, NV, ROWS, NZ),
             vmem(2, NV, NY, LANES),
             dma(NX + 3),
             dma(2, 2, CH),
             dma(2, 2, CH),
+            dma(2, 2),
+            dma(2, 2),
             dma(2, 2, 2),
             dma(2, 2, 2),
             dma(sum(counts)),
@@ -588,7 +632,7 @@
     return pl.pallas_call(
         finish,
         out_shape=(array(*block), array(*block)),
-        in_specs=[in_vmem] * 5,
+        in_specs=[in_vmem] * 6,
         out_specs=[in_hbm] * 2,
         scratch_shapes=[vmem(2, 2, NV, NY, NZ), dma(2, 3)],
         compiler_params=pltpu.CompilerParams(vmem_limit_bytes=16 * 2**20),

time: 35.4 us -> 34.5 us (0.975)
  Pallas kernels: 34.7 us -> 33.7 us
    pallas_call x1, Pallas kernels: 33.3 us -> 32.4 us  [shards(): pl.pallas_call(functools.partial(kernel, sizes), out_shape=(array(*block)...]
where the time goes in v4:
time: 34.5 us; the launch traced here: 34.4 us
  Pallas kernels  33.7 us (98%)
  between operations  0.64 us (2%)
    pallas_call x1, Pallas kernels, shards(): pl.pallas_call(functools.partial(kernel, sizes), out_shape=(array(*block)...  32.4 us
    pallas_call x1, Pallas kernels, shards(): pl.pallas_call(finish, out_shape=(array(*block), array(*block)), in_specs...  1.4 us

profile of v4, /device:TPU:1, one launch (start us, length us, event | category | flops | bytes accessed | tf_op | source)
XLA Modules:
  0.0 34.4 jit_solution(17859248875231174266)
XLA Ops:
  0.6 32.4 %sections.1 = (f32[5,6,24,384]{3,2,1,0:T(8,128)S(1)}, f32[5,6,24,384]{3,2,1,0:T(8,128)S(1)}, f32[2,5,24,384]{3,2,1,0:T(8,128)S(1)}, f32[2,2,5,8,384]{4,3,2,1,0:T...) custom-call(f32[5,6,24,384]{3,2,1,0:T(8,128)} %state.1, f32[5,6,24,384]{3,2,1,0:T(8,128)} %register.1, ...), custom_call_target="tpu_custom_call" | custom-call | tf_op jit(solution)/shard_map/sections/pallas_call | solution.py:585
  33.0 1.4 %finish.1 = (f32[5,6,24,384]{3,2,1,0:T(8,128)}, f32[5,6,24,384]{3,2,1,0:T(8,128)}) custom-call(f32[5,6,24,384]{3,2,1,0:T(8,128)S(1)} %get-tuple-element.8.u, f32[5,6,24,384]{3,2,1,0:T(8,128)S(1)} %get-tuple-element.9.k, f32[2,5,24,384]{3,2,1,0:T(8,128)S(1)} %get-tuple-element.10.edge, f32[2,2,5,8,384]{4,3,2,1,0:T(8,128)S(1)} %get-tuple-element.11.far_x, ...), custom_call_target="tpu_custom_call" | custom-call | tf_op jit(solution)/shard_map/finish/pallas_call | solution.py:632

commit v5 on v4

--- a/solution.py
+++ b/solution.py
@@ -27,6 +27,7 @@
 ROWS = 8
 CH = NY // ROWS
 LANES = 128
+AHEAD = 2 * LANES
 SCALE = 2.0 / ELEM_WIDTH
 FACE = SCALE * 15.0 * 0.5
 
@@ -133,6 +134,7 @@
     k,
     edge,
     far_x,
+    far_rest,
     far_ab,
     step,
     res,
@@ -263,7 +265,7 @@
             return low, high
 
         ones = jnp.ones((NY, LANES), jnp.float32)
-        low, high = lax.fori_loop(0, NV, body, (ones, ones))
+        low, high = lax.fori_loop(0, NV, body, (ones, ones), unroll=True)
         z_pack[sec, 0] = low
         z_pack[sec, 1] = high
 
@@ -277,11 +279,17 @@
             device_id_type=MESH,
         )
 
+    def plane(side):
+        return 0 if side == 0 else NX - 1
+
     def x_copy(sec, side, c):
-        src = state if sec == 0 else u
+        lanes = pl.ds(AHEAD, NZ - AHEAD) if sec and c == 0 else pl.ds(0, NZ)
+        slots = near_x.at[1 - side, c]
+        if sec:
+            slots = far_x.at[1 - side, c - 1] if c else far_rest.at[1 - side]
         return remote(
-            src.at[:, 0 if side == 0 else NX - 1, pl.ds(ROWS * c, ROWS), :],
-            far_x.at[1 - side, c - 1] if sec else near_x.at[1 - side, c],
+            (u if sec else state).at[:, plane(side), pl.ds(ROWS * c, ROWS), lanes],
+            slots,
             send_x.at[sec, side, c],
             recv_x.at[sec, 1 - side, c],
             gx[side],
@@ -382,7 +390,7 @@
             res[v] = res[v] + (both + along_y).reshape(NX, NY, NZ)
             return carry
 
-        lax.fori_loop(0, NV, body, 0)
+        lax.fori_loop(0, NV, body, 0, unroll=True)
 
     def lines_x():
         half = N // 2
@@ -402,7 +410,7 @@
                     res[v, N - 1 - i, rows, :] += b - a
             return carry
 
-        lax.fori_loop(0, NV, body, 0)
+        lax.fori_loop(0, NV, body, 0, unroll=True)
 
     def y_z_faces(sec):
         for side in (0, 1):
@@ -434,7 +442,7 @@
                 res[v, x, :, NZ - LANES : NZ] += jnp.where(lane_1 == LANES - 1, high, 0.0)
             return carry
 
-        lax.fori_loop(0, NV, body, 0)
+        lax.fori_loop(0, NV, body, 0, unroll=True)
 
     def update(sec, x, c, extra):
         rows = pl.ds(ROWS * c, ROWS)
@@ -446,14 +454,13 @@
             k[v, x, rows, :] = new_k
             u[v, x, rows, :] = new_u
 
-    def plane(side):
-        return 0 if side == 0 else NX - 1
-
     def known_part(side):
         a, b = COEFFS[0]
         rows = pl.ds(0, ROWS)
         for v in range(NV):
-            ab[0, side, v] = u[v, plane(side), rows, :] + b * (a * k[v, plane(side), rows, :])
+            ab[0, side, v] = u[v, plane(side), rows, 0:AHEAD] + b * (
+                a * k[v, plane(side), rows, 0:AHEAD]
+            )
         ab_copy(0, side).start()
 
     def step_part(side):
@@ -461,7 +468,7 @@
         for v in range(NV):
             r = res[v, plane(side), 0:ROWS, :] + extra[v]
             res[v, plane(side), 0:ROWS, :] = r
-            ab[1, side, v] = COEFFS[0][1] * r
+            ab[1, side, v] = COEFFS[0][1] * r[:, :AHEAD]
         ab_copy(1, side).start()
 
     def boundary_terms(side, c):
@@ -502,10 +509,10 @@
     value = jnp.max(jnp.broadcast_to(value, (ROWS, LANES)), axis=1, keepdims=True)
     step[...] = jnp.broadcast_to(COURANT * ELEM_WIDTH / (11.0 * value), (ROWS, NZ))
 
-    for c in (*range(1, CH), 0):
+    for c in (1, 0, *range(2, CH)):
         for side in (0, 1):
             update(0, plane(side), c, boundary_terms(side, c) if c else None)
-            if 0 < c < CH - 1:
+            if c < CH - 1:
                 x_copy(1, side, c).start()
     update_interior(0)
     pack(1)
@@ -523,7 +530,7 @@
     for side in (0, 1):
         for part in (0, 1):
             ab_copy(part, side).wait_recv()
-        for c in range(1, CH):
+        for c in range(CH):
             x_copy(1, side, c).wait_recv()
 
     for copy in tops_1 + tops_2 + tops_3:
@@ -533,11 +540,11 @@
             copy.wait_send()
         for side in (0, 1):
             ab_copy(sec, side).wait_send()
-            for c in range(sec, CH):
+            for c in range(CH):
                 x_copy(sec, side, c).wait_send()
 
 
-def finish(u, k, edge, far_x, far_ab, step, out_state, out_register, done, sem):
+def finish(u, k, edge, far_x, far_rest, far_ab, step, out_state, out_register, done, sem):
     inner = [
         pltpu.make_async_copy(
             src.at[:, pl.ds(1, NX - 2)], dst.at[:, pl.ds(1, NX - 2)], sem.at[i, 0]
@@ -555,7 +562,13 @@
             if c:
                 far = [far_x[side, c - 1, v] for v in range(NV)]
             else:
-                far = [far_ab[0, side, v] + step[...] * far_ab[1, side, v] for v in range(NV)]
+                dt = step[:, 0:AHEAD]
+                far = [
+                    jnp.concatenate(
+                        [far_ab[0, side, v] + dt * far_ab[1, side, v], far_rest[side, v]], axis=1
+                    )
+                    for v in range(NV)
+                ]
             extra = x_face(side, own, far)
             for v in range(NV):
                 new_k, new_u = advance(
@@ -589,11 +602,12 @@
             array(*block),
             array(2, NV, NY, NZ),
             array(2, CH - 1, NV, ROWS, NZ),
-            array(2, 2, NV, ROWS, NZ),
+            array(2, NV, ROWS, NZ - AHEAD),
+            array(2, 2, NV, ROWS, AHEAD),
             array(ROWS, NZ),
         ),
         in_specs=[in_hbm] * 4,
-        out_specs=[in_vmem] * 6,
+        out_specs=[in_vmem] * 7,
         scratch_shapes=[
             vmem(*block),
             vmem(*block),
@@ -611,7 +625,7 @@
             vmem(2, 2, NV, ROWS, NZ),
             vmem(2, 2, NY, LANES),
             vmem(2, CH, NV, ROWS, NZ),
-            vmem(2, 2, NV, ROWS, NZ),
+            vmem(2, 2, NV, ROWS, AHEAD),
             vmem(2, NV, ROWS, NZ),
             vmem(2, NV, NY, LANES),
             dma(NX + 3),
@@ -632,7 +646,7 @@
     return pl.pallas_call(
         finish,
         out_shape=(array(*block), array(*block)),
-        in_specs=[in_vmem] * 6,
+        in_specs=[in_vmem] * 7,
         out_specs=[in_hbm] * 2,
         scratch_shapes=[vmem(2, 2, NV, NY, NZ), dma(2, 3)],
         compiler_params=pltpu.CompilerParams(vmem_limit_bytes=16 * 2**20),

time: 34.5 us -> 34.3 us (level)
  no operation moved by 1% of the time
where the time goes in v5:
time: 34.3 us; the launch traced here: 34.2 us
  Pallas kernels  33.6 us (98%)
  between operations  0.64 us (2%)
    pallas_call x1, Pallas kernels, shards(): pl.pallas_call(functools.partial(kernel, sizes), out_shape=(array(*block)...  32.2 us
    pallas_call x1, Pallas kernels, shards(): pl.pallas_call(finish, out_shape=(array(*block), array(*block)), in_specs...  1.4 us

profile of v5, /device:TPU:1, one launch (start us, length us, event | category | flops | bytes accessed | tf_op | source)
XLA Modules:
  0.0 34.2 jit_solution(4675202889389975515)
XLA Ops:
  0.6 32.2 %sections.1 = (f32[5,6,24,384]{3,2,1,0:T(8,128)S(1)}, f32[5,6,24,384]{3,2,1,0:T(8,128)S(1)}, f32[2,5,24,384]{3,2,1,0:T(8,128)S(1)}, f32[2,2,5,8,384]{4,3,2,1,0:T...) custom-call(f32[5,6,24,384]{3,2,1,0:T(8,128)} %state.1, ...), custom_call_target="tpu_custom_call" | custom-call | tf_op jit(solution)/shard_map/sections/pallas_call | solution.py:598
  32.8 1.4 %finish.1 = (f32[5,6,24,384]{3,2,1,0:T(8,128)}, f32[5,6,24,384]{3,2,1,0:T(8,128)}) custom-call(f32[5,6,24,384]{3,2,1,0:T(8,128)S(1)} %get-tuple-element.9.u, f32[5,6,24,384]{3,2,1,0:T(8,128)S(1)} %get-tuple-element.10.k, f32[2,5,24,384]{3,2,1,0:T(8,128)S(1)} %get-tuple-element.11.edge, f32[2,2,5,8,384]{4,3,2,1,0:T(8,128)S(1)} %get-tuple-element.12.far_x, ...), custom_call_target="tpu_custom_call" | custom-call | tf_op jit(solution)/shard_map/finish/pallas_call | solution.py:646

commit v6 on v5

--- a/solution.py
+++ b/solution.py
@@ -489,6 +489,9 @@
     pack(0)
     start(y_z_copies(0))
     fluxes_and_jumps()
+    loads[0].wait()
+    loads[1].wait()
+    lines_y_z()
     top[1] = gather_top(0, tops_1, top_1)
     start(tops_2)
     for c in range(1, CH):
@@ -496,9 +499,6 @@
     loads[2].wait()
     for side in (0, 1):
         known_part(side)
-    loads[0].wait()
-    loads[1].wait()
-    lines_y_z()
     top[2] = gather_top(1, tops_2, top_2)
     start(tops_3)
     lines_x()
@@ -512,12 +512,11 @@
     for c in (1, 0, *range(2, CH)):
         for side in (0, 1):
             update(0, plane(side), c, boundary_terms(side, c) if c else None)
-            if c < CH - 1:
-                x_copy(1, side, c).start()
     update_interior(0)
     pack(1)
     start(y_z_copies(1))
-    start([x_copy(1, 0, CH - 1), x_copy(1, 1, CH - 1)])
+    for c in (1, 0, *range(2, CH)):
+        start([x_copy(1, 0, c), x_copy(1, 1, c)])
 
     fluxes_and_jumps()
     lines_y_z()

time: 34.3 us -> 33.4 us (0.974)
  Pallas kernels: 33.6 us -> 32.6 us
    pallas_call x1, Pallas kernels: 32.2 us -> 31.2 us  [shards(): pl.pallas_call(functools.partial(kernel, sizes), out_shape=(array(*block)...]
where the time goes in v6:
time: 33.4 us; the launch traced here: 33.2 us
  Pallas kernels  32.6 us (98%)
  between operations  0.64 us (2%)
    pallas_call x1, Pallas kernels, shards(): pl.pallas_call(functools.partial(kernel, sizes), out_shape=(array(*block)...  31.2 us
    pallas_call x1, Pallas kernels, shards(): pl.pallas_call(finish, out_shape=(array(*block), array(*block)), in_specs...  1.4 us

profile of v6, /device:TPU:1, one launch (start us, length us, event | category | flops | bytes accessed | tf_op | source)
XLA Modules:
  0.0 33.2 jit_solution(11623780876398466135)
XLA Ops:
  0.6 31.2 %sections.1 = (f32[5,6,24,384]{3,2,1,0:T(8,128)S(1)}, f32[5,6,24,384]{3,2,1,0:T(8,128)S(1)}, f32[2,5,24,384]{3,2,1,0:T(8,128)S(1)}, f32[2,2,5,8,384]{4,3,2,1,0:T...) custom-call(f32[5,6,24,384]{3,2,1,0:T(8,128)} %state.1, ...), custom_call_target="tpu_custom_call" | custom-call | tf_op jit(solution)/shard_map/sections/pallas_call | solution.py:597
  31.8 1.4 %finish.1 = (f32[5,6,24,384]{3,2,1,0:T(8,128)}, f32[5,6,24,384]{3,2,1,0:T(8,128)}) custom-call(f32[5,6,24,384]{3,2,1,0:T(8,128)S(1)} %get-tuple-element.9.u, f32[5,6,24,384]{3,2,1,0:T(8,128)S(1)} %get-tuple-element.10.k, f32[2,5,24,384]{3,2,1,0:T(8,128)S(1)} %get-tuple-element.11.edge, f32[2,2,5,8,384]{4,3,2,1,0:T(8,128)S(1)} %get-tuple-element.12.far_x, ...), custom_call_target="tpu_custom_call" | custom-call | tf_op jit(solution)/shard_map/finish/pallas_call | solution.py:645
